TPU v7x, 8 devices: a whole 2x2x1 slice. The times are simulated.
8 devices in a mesh: dp: 1 (over z), vblk: 2 (over y), vocab: 4 (over x, core).
Axes of the slice: x: 2, y: 2, z: 1, core: 2. Of those that a mesh axis runs over, the one named last changes fastest.
Arguments:
- hidden: bfloat16 [1024, 4096], P('dp')
- w_head: bfloat16 [4096, 32768], P(None, ('vblk', 'vocab'))
- inv_temp: float32 [1024], P('dp')
- target: int32 [1024], P('dp')
Outputs:
- output 1: float32 [1024, 32768], P('dp', ('vblk', 'vocab'))
- output 2: float32 [1024], P('dp')
All inputs are finite; a program needn't handle non-finite values.
Results may differ from a plain program's by a relative error of at most 0.001.
Values are sent between devices in bfloat16 or wider.
A program may use at most 1 GiB of HBM per device.

v0:
```python
import jax
import jax.numpy as jnp
from jax import lax
from jax.sharding import PartitionSpec as P


def solution(mesh):
    vocab_axes = ("vblk", "vocab")
    vocab_size = mesh.shape["vocab"]
    shard_count = mesh.shape["vblk"] * vocab_size

    def local_step(hidden, w_head, inv_temp, target):
        shard_width = w_head.shape[1]
        shard_idx = lax.axis_index("vblk") * vocab_size + lax.axis_index("vocab")
        logits = jnp.dot(hidden, w_head, preferred_element_type=jnp.float32) * inv_temp[:, None]
        local_max = jnp.max(logits, axis=1)
        exp_val = jnp.exp(logits - local_max[:, None])
        local_sum = jnp.sum(exp_val, axis=1)
        stat_pairs = lax.all_gather(jnp.stack([local_max, local_sum]), vocab_axes)
        glob_max = jnp.max(stat_pairs[:, 0], axis=0)
        glob_sum = jnp.sum(stat_pairs[:, 1] * jnp.exp(stat_pairs[:, 0] - glob_max[None, :]), axis=0)
        rescale = jnp.exp(local_max - glob_max) / glob_sum
        cdf_loc = jnp.cumsum(exp_val * rescale[:, None], axis=1)
        totals = lax.all_gather(cdf_loc[:, -1], vocab_axes)
        lower_shard = jnp.arange(shard_count) < shard_idx
        offset = jnp.sum(jnp.where(lower_shard[:, None], totals, 0.0), axis=0)
        cdf_table = cdf_loc + offset[:, None]
        col_ids = shard_idx * shard_width + jnp.arange(shard_width)
        is_target = col_ids[None, :] == target[:, None]
        picked = lax.psum(jnp.sum(jnp.where(is_target, cdf_table, 0.0), axis=1), vocab_axes)
        return cdf_table, picked

    return jax.shard_map(local_step, mesh=mesh, in_specs=(P("dp", None), P(None, vocab_axes), P("dp"), P("dp")), out_specs=(P("dp", vocab_axes), P("dp")), check_vma=False)
```

profile of v0, /device:TPU:0, one launch (start us, length us, event | category | flops | bytes accessed | tf_op | source)
XLA Modules:
  0.0 201.5 jit_solution(2877503216965613188)
XLA Ops:
  0.6 0.0 copy-start.1
  0.6 43.4 %multiply_reduce_fusion = (f32[1024]{0:T(1024)S(1)}, f32[1024,4096]{1,0:T(8,128)S(1)}) fusion(f32[1024]{0:T(1024)} %param.6, bf16[1024,4096]{1,0:T(8,128)(2,1)} %param.4, bf16[4096,4096]{1,0:T(8,128)(2,1)} %param.5), kind=kOutput, calls=%fused_computation.3 | convolution fusion | flops 34368126976 | bytes 58728448 | tf_op jit(solution)/shard_map/dot_general | solution.py:15
  44.0 0.0 copy-done.1
  44.0 3.5 %fusion = f32[1024]{0:T(1024)S(1)} fusion(f32[1024,4096]{1,0:T(8,128)S(1)} %get-tuple-element.10, f32[1024]{0:T(1024)S(1)} %get-tuple-element.9, f32[1024]{0:T(1024)S(1)} %copy-done.1), kind=kLoop, calls=%fused_computation.4 | loop fusion | flops 12581888 | bytes 16789504 | tf_op jit(solution)/shard_map/reduce_sum | solution.py:18
  47.6 13.9 %all-gather.2 = f32[8,2,1024]{2,1,0:T(2,128)S(1)} all-gather(f32[1,2,1024]{2,1,0:T(2,128)S(1)} %maximum_bitcast_fusion), channel_id=2, replica_groups=mesh['dp'=1,'vblk'=2,'vocab'=4] {'vblk','vocab'}, dimensions={0}, use_global_device_ids=true | all-gather | bytes 73728 | tf_op jit(solution)/shard_map/all_gather | solution.py:19
  61.5 0.1 slice_reduce_fusion
  61.6 4.6 %multiply_bitcast_fusion = f32[128,8,32,128]{3,1,2,0:T(8,128)S(1)} fusion(f32[1024,4096]{1,0:T(8,128)S(1)} %get-tuple-element.10, f32[1024]{0:T(1024)S(1)} %exponential_divide_fusion, f32[1024]{0:T(1024)S(1)} %get-tuple-element.9, f32[1024]{0:T(1024)S(1)} %copy-done.1), kind=kLoop, calls=%fused_computation.1 | loop fusion | flops 12582912 | bytes 33566720
  66.2 7.1 %copy.18 = f32[128,8,32,128]{3,2,1,0:T(8,128)} copy(f32[128,8,32,128]{3,1,2,0:T(8,128)S(1)} %multiply_bitcast_fusion) | data formatting | bytes 33554432
  73.3 16.5 %copy.13 = f32[1024,32,128]{0,1,2:T(8,128)} copy(f32[1024,32,128]{2,1,0:T(8,128)} %bitcast.28) | data formatting | bytes 33554432 | tf_op jit(solution)/shard_map/reshape
  89.8 12.4 %fusion.4 = f32[1024,32,128]{0,1,2:T(8,128)} fusion(f32[1024,32,128]{0,1,2:T(8,128)} %copy.13), kind=kOutput, calls=%fused_computation.19 | output fusion | flops 532676608 | bytes 33554432 | tf_op jit(solution)/shard_map/reduce-window
  102.2 0.9 slice_bitcast_fusion
  103.2 0.1 reduce-window.9
  103.3 6.8 %broadcast_add_fusion.1 = f32[1024,32,128]{0,1,2:T(8,128)S(1)} fusion(f32[1024,32,128]{0,1,2:T(8,128)} %fusion.4, f32[1024,32]{0,1:T(8,128)S(1)} %slice.24), kind=kLoop, calls=%fused_computation.6 | loop fusion | flops 4194304 | bytes 33685504 | tf_op jit(solution)/shard_map/reduce_window_sum
  110.1 0.0 copy-start.2
  110.2 14.7 %copy.14 = f32[1024,32,128]{0,2,1:T(8,128)S(1)} copy(f32[1024,32,128]{0,1,2:T(8,128)S(1)} %broadcast_add_fusion.1) | data formatting | bytes 33554432 | tf_op jit(solution)/shard_map/reduce_window_sum
  124.9 0.0 copy-start
  124.9 5.7 %copy-done = f32[1024,32,128]{0,2,1:T(8,128)} copy-done((f32[1024,32,128]{0,2,1:T(8,128)}, f32[1024,32,128]{0,2,1:T(8,128)S(1)}, u32[]{:S(2)}) %copy-start) | copy-done | bytes 16777240
  130.6 11.0 %all-gather.1 = f32[8192,1]{0,1:T(1,128)S(1)} all-gather(f32[1024,1]{0,1:T(1,128)S(1)} %slice.25), channel_id=3, replica_groups=mesh['dp'=1,'vblk'=2,'vocab'=4] {'vblk','vocab'}, dimensions={0}, use_global_device_ids=true | all-gather | bytes 36864 | tf_op jit(solution)/shard_map/all_gather | solution.py:24
  141.6 0.5 broadcast.36
  142.1 0.7 reduce.5
  142.9 0.1 select_reduce_fusion.1
  143.0 0.0 copy-done.2
  143.0 7.4 %select_reduce_fusion = f32[1024]{0:T(1024)S(1)} fusion(f32[1024]{0:T(1024)S(1)} %select_reduce_fusion.1, s32[1024]{0:T(1024)S(1)} %copy-done.2, s32[32,128]{0,1:T(8,128)S(1)} %add_add_fusion, f32[1024,32,128]{0,1,2:T(8,128)} %fusion.4, f32[1024,32]{0,1:T(8,128)S(1)} %slice.24), kind=kLoop, calls=%fused_computation | loop fusion | flops 20970496 | bytes 16936960 | tf_op jit(solution)/shard_map/reduce_sum | solution.py:30
  150.4 22.3 %psum.7 = f32[1024]{0:T(1024)} all-reduce(f32[1024]{0:T(1024)S(1)} %select_reduce_fusion), channel_id=1, replica_groups=mesh['dp'=1,'vblk'=2,'vocab'=4] {'vblk','vocab'}, use_global_device_ids=true, to_apply=%region_8.9 | all-reduce | flops 1024 | bytes 8192 | tf_op jit(solution)/shard_map/psum | solution.py:30
  172.6 11.4 %broadcast_add_fusion = f32[1024,4096]{0,1:T(8,128)} fusion(f32[1024]{0:T(1024)S(1)} %select_reduce_fusion.1, f32[1024,32,128]{0,2,1:T(8,128)} %copy-done), kind=kLoop, calls=%fused_computation.5 | loop fusion | flops 4194304 | bytes 33558528 | tf_op jit(solution)/shard_map/add | solution.py:27
  184.1 17.4 %copy.15 = f32[1024,4096]{1,0:T(8,128)} copy(f32[1024,4096]{0,1:T(8,128)} %broadcast_add_fusion) | data formatting | bytes 33554432
  (8 shorter events, 0.1 us)
Async XLA Ops:
  0.6 43.4 %copy-start.1 = (f32[1024]{0:T(1024)S(1)}, f32[1024]{0:T(1024)}, u32[]{:S(2)}) copy-start(f32[1024]{0:T(1024)} %param.6) | copy-start | bytes 12292
  110.1 32.8 %copy-start.2 = (s32[1024]{0:T(1024)S(1)}, s32[1024]{0:T(1024)}, u32[]{:S(2)}) copy-start(s32[1024]{0:T(1024)} %param.7) | copy-start | bytes 12292
  124.9 5.7 %copy-start = (f32[1024,32,128]{0,2,1:T(8,128)}, f32[1024,32,128]{0,2,1:T(8,128)S(1)}, u32[]{:S(2)}) copy-start(f32[1024,32,128]{0,2,1:T(8,128)S(1)} %copy.14) | copy-start | bytes 50331652
where the time goes:
time: 202 us; the launch traced here: 201 us
  local copies, waits for them, and re-layouts  63 us (31%)
  other arithmetic  47.2 us (23%)
  blocking collectives  47.1 us (23%)
  matrix products  43.4 us (21%)
    dot_general x1, matrix products, local_step(): jnp.dot(hidden, w_head, preferred_element_type=jnp.float32)  43.4 us
    unnamed x8, local copies, waits for them, and re-layouts  30.3 us
    psum x1, blocking collectives, local_step(): lax.psum(jnp.sum(jnp.where(is_target, cdf_table, 0.0), axis=1), vocab_axes)  22.3 us
    another operation x3, other arithmetic  19.3 us
    reshape x1, local copies, waits for them, and re-layouts  16.5 us
    another operation x3, local copies, waits for them, and re-layouts  15.7 us
    all_gather x1, blocking collectives, local_step(): stat_pairs = lax.all_gather(jnp.stack([local_max, local_sum]), vocab_axes)  13.9 us
    add x1, other arithmetic, local_step(): cdf_table = cdf_loc + offset[:, None]  11.4 us

commit v1 on v0

v1 whole, which is shorter than its diff:
```python
import functools
import math

import jax
import jax.numpy as jnp
from jax import lax
from jax.experimental import pallas as pl
from jax.experimental.pallas import tpu as pltpu
from jax.sharding import PartitionSpec as P

MESH = pl.DeviceIdType.MESH
VMEM = pl.BlockSpec(memory_space=pltpu.VMEM)
ANY = pl.BlockSpec(memory_space=pl.ANY)
LOG2E = math.log2(math.e)
BLOCK = 512
UNIT = 256
OUT_ROWS = 64
RING = 4


def block_prefix(logits, prefix, stats, block, row0, tau2, rel):
    sub = lax.broadcasted_iota(jnp.int32, (8, 128), 0)
    for s in range(0, UNIT, 128):
        lanes = pl.ds(row0 + s, 128)
        tiles = []
        for t in range(0, BLOCK, 128):
            turned = logits[s : s + 128, t : t + 128].T
            tiles += [turned[i : i + 8] for i in range(0, 128, 8)]
        top = functools.reduce(jnp.maximum, tiles)
        top = jnp.max(top, axis=0, keepdims=True)
        scale = tau2[0:1, lanes]
        where_tgt = rel[0:1, lanes] - block * BLOCK - sub
        carry = None
        hit = jnp.zeros((8, 128), jnp.float32)
        out = []
        for i, tile in enumerate(tiles):
            e = jnp.exp2((tile - top) * scale)
            for k in (1, 2, 4):
                e = e + jnp.where(sub >= k, pltpu.roll(e, k, 0), 0.0)
            if carry is not None:
                e = e + carry
            carry = e[7:8, :]
            hit = jnp.where(where_tgt == 8 * i, e, hit)
            out.append(e)
        here = sub == block
        for q, value in enumerate((top, carry, jnp.sum(hit, axis=0, keepdims=True))):
            stats[q, :, lanes] = jnp.where(here, value, stats[q, :, lanes])
        per = 128 // 8
        for t in range(BLOCK // 128):
            col = jnp.concatenate(out[per * t : per * (t + 1)], axis=0)
            prefix[block, pl.ds(row0 + s, 128), t * 128 : (t + 1) * 128] = col.T


def main_kernel(h_hbm, w_hbm, tau_ref, tgt_ref, prefix, stats, hbuf, wbuf, z0, z1, tau2, rel, hsem, wsem):
    rows = h_hbm.shape[0]
    width = w_hbm.shape[1]
    units = rows // UNIT
    blocks = width // BLOCK
    zs = (z0, z1)
    me = lax.axis_index("vblk") * lax.axis_size("vocab") + lax.axis_index("vocab")

    def w_copy(c):
        cols = pl.ds(pl.multiple_of(c * BLOCK, BLOCK), BLOCK)
        slot = lax.rem(c, 2)
        return pltpu.make_async_copy(w_hbm.at[:, cols], wbuf.at[slot], wsem.at[slot])

    def h_copy(r):
        part = pl.ds(r * UNIT, UNIT)
        return pltpu.make_async_copy(h_hbm.at[part], hbuf.at[part], hsem.at[r])

    h_copy(0).start()
    w_copy(0).start()
    for r in range(1, units):
        h_copy(r).start()
    tau2[...] = tau_ref[...] * LOG2E
    rel[...] = tgt_ref[...] - me * width
    stats[...] = jnp.zeros_like(stats)
    z1[...] = jnp.zeros_like(z1)
    for r in range(units):
        h_copy(r).wait()

    def body(c, _):
        w_copy(c).wait()

        @pl.when(c + 1 < blocks)
        def _():
            w_copy(c + 1).start()

        w = wbuf.at[lax.rem(c, 2)]
        for r in range(units):
            zs[r % 2][...] = jnp.dot(hbuf[r * UNIT : (r + 1) * UNIT, :], w[...], preferred_element_type=jnp.float32)
            before = zs[(r + 1) % 2]
            if r == 0:
                block_prefix(before, prefix, stats, lax.rem(c + blocks - 1, blocks), rows - UNIT, tau2, rel)
            else:
                block_prefix(before, prefix, stats, c, (r - 1) * UNIT, tau2, rel)
        return 0

    lax.fori_loop(0, blocks, body, 0)
    block_prefix(zs[(units - 1) % 2], prefix, stats, blocks - 1, rows - UNIT, tau2, rel)


def sublane_scan(x):
    sub = lax.broadcasted_iota(jnp.int32, x.shape, 0)
    for k in (1, 2, 4):
        x = x + jnp.where(sub >= k, pltpu.roll(x, k, 0), 0.0)
    return x


def exchange_kernel(width, stats, tau_ref, tgt_ref, coef, picked, mine, theirs, send_sem, recv_sem):
    vocab = lax.axis_size("vocab")
    n = lax.axis_size("vblk") * vocab
    me = lax.axis_index("vblk") * vocab + lax.axis_index("vocab")
    rows = stats.shape[2]
    groups = rows // 128

    def device(d):
        k = lax.rem(me + d, n)
        return {"vblk": k // vocab, "vocab": lax.rem(k, vocab)}

    barrier = pltpu.get_barrier_semaphore()
    for d in range(1, n):
        pl.semaphore_signal(barrier, inc=1, device_id=device(d), device_id_type=MESH)

    tau2 = tau_ref[...] * LOG2E
    top = stats[0]
    best = jnp.max(top, axis=0, keepdims=True)
    weight = jnp.exp2((top - best) * tau2)
    mass = stats[1] * weight
    upto = sublane_scan(mass)
    sub = lax.broadcasted_iota(jnp.int32, upto.shape, 0)
    below = jnp.where(sub == 0, 0.0, pltpu.roll(upto, 1, 0))
    total = upto[7:8, :]
    rel = tgt_ref[...] - me * width
    inside = (rel >= sub * BLOCK) & (rel < (sub + 1) * BLOCK)
    at_tgt = jnp.sum(jnp.where(inside, below + stats[2] * weight, 0.0), axis=0, keepdims=True)
    for q, value in enumerate((best, total, at_tgt)):
        for g in range(groups):
            mine[q, g : g + 1, :] = value[:, g * 128 : (g + 1) * 128]
            theirs[me, q, g : g + 1, :] = value[:, g * 128 : (g + 1) * 128]

    pl.semaphore_wait(barrier, n - 1)
    copies = []
    for d in range(1, n):
        copy = pltpu.make_async_remote_copy(
            src_ref=mine,
            dst_ref=theirs.at[me],
            send_sem=send_sem.at[d - 1],
            recv_sem=recv_sem.at[d - 1],
            device_id=device(d),
            device_id_type=MESH,
        )
        copy.start()
        copies.append(copy)
    for copy in copies:
        copy.wait()

    def compact(ref):
        x = ref[...]
        return jnp.concatenate([x[:, g * 128 : (g + 1) * 128] for g in range(groups)], axis=0)

    t2 = compact(tau_ref) * LOG2E
    owner = compact(tgt_ref) // width
    high = functools.reduce(jnp.maximum, [theirs[k, 0] for k in range(n)])
    masses = []
    grand = low = pick = jnp.zeros((groups, 128), jnp.float32)
    for k in range(n):
        factor = jnp.exp2((theirs[k, 0] - high) * t2)
        part = theirs[k, 1] * factor
        grand = grand + part
        low = low + jnp.where(k < me, part, 0.0)
        pick = pick + jnp.where(k < owner, part, 0.0) + theirs[k, 2] * factor
    inverse = 1.0 / grand
    own = jnp.exp2((mine[0] - high) * t2) * inverse
    low = low * inverse
    picked[...] = pick * inverse
    for g in range(groups):
        cols = slice(g * 128, (g + 1) * 128)
        scale = weight[:, cols] * own[g : g + 1, :]
        offset = low[g : g + 1, :] + below[:, cols] * own[g : g + 1, :]
        coef[g * 128 : (g + 1) * 128, 0:16] = jnp.concatenate([scale, offset], axis=0).T


def finish_kernel(prefix, coef, picked, out_hbm, picked_out, ring, sem):
    blocks = prefix.shape[0]
    rows = prefix.shape[1]
    picked_out[...] = picked[...]

    def copy(i, slot):
        part = pl.ds(pl.multiple_of(i * OUT_ROWS, OUT_ROWS), OUT_ROWS)
        return pltpu.make_async_copy(ring.at[slot], out_hbm.at[part], sem.at[slot])

    def body(j, _):
        for slot in range(RING):
            i = j * RING + slot

            @pl.when(j > 0)
            def _():
                copy(i - RING, slot).wait()

            for s in range(0, OUT_ROWS, 8):
                part = pl.ds(pl.multiple_of(i * OUT_ROWS + s, 8), 8)
                c = coef[part, 0:16]
                for b in range(blocks):
                    x = prefix[b, part, :]
                    ring[slot, s : s + 8, b * BLOCK : (b + 1) * BLOCK] = x * c[:, b : b + 1] + c[:, 8 + b : 9 + b]
            copy(i, slot).start()
        return 0

    steps = rows // OUT_ROWS // RING
    lax.fori_loop(0, steps, body, 0)
    for slot in range(RING):
        copy((steps - 1) * RING + slot, slot).wait()


def solution(mesh):
    vocab_axes = ("vblk", "vocab")

    def local_step(hidden, w_head, inv_temp, target):
        rows, depth = hidden.shape
        width = w_head.shape[1]
        blocks = width // BLOCK
        n = mesh.shape["vblk"] * mesh.shape["vocab"]
        tau = inv_temp.reshape(1, rows)
        tgt = target.reshape(1, rows)
        prefix, stats = pl.pallas_call(
            main_kernel,
            out_shape=(
                pltpu.VMEM((blocks, rows, BLOCK), jnp.float32),
                pltpu.VMEM((3, blocks, rows), jnp.float32),
            ),
            in_specs=[ANY, ANY, VMEM, VMEM],
            out_specs=(VMEM, VMEM),
            scratch_shapes=[
                pltpu.VMEM((rows, depth), jnp.bfloat16),
                pltpu.VMEM((2, depth, BLOCK), jnp.bfloat16),
                pltpu.VMEM((UNIT, BLOCK), jnp.float32),
                pltpu.VMEM((UNIT, BLOCK), jnp.float32),
                pltpu.VMEM((1, rows), jnp.float32),
                pltpu.VMEM((1, rows), jnp.int32),
                pltpu.SemaphoreType.DMA((rows // UNIT,)),
                pltpu.SemaphoreType.DMA((2,)),
            ],
            compiler_params=pltpu.CompilerParams(vmem_limit_bytes=44 << 20),
            name="logits_prefix",
        )(hidden, w_head, tau, tgt)
        coef, picked = pl.pallas_call(
            functools.partial(exchange_kernel, width),
            out_shape=(
                pltpu.VMEM((rows, 128), jnp.float32),
                pltpu.VMEM((rows // 128, 128), jnp.float32),
            ),
            in_specs=[VMEM, VMEM, VMEM],
            out_specs=(VMEM, VMEM),
            scratch_shapes=[
                pltpu.VMEM((3, rows // 128, 128), jnp.float32),
                pltpu.VMEM((n, 3, rows // 128, 128), jnp.float32),
                pltpu.SemaphoreType.DMA((n - 1,)),
                pltpu.SemaphoreType.DMA((n - 1,)),
            ],
            compiler_params=pltpu.CompilerParams(
                vmem_limit_bytes=16 << 20, collective_id=0, has_side_effects=True
            ),
            name="exchange",
        )(stats, tau, tgt)
        table, picked = pl.pallas_call(
            finish_kernel,
            out_shape=(
                jax.ShapeDtypeStruct((rows, width), jnp.float32),
                jax.ShapeDtypeStruct((rows // 128, 128), jnp.float32),
            ),
            in_specs=[VMEM, VMEM, VMEM],
            out_specs=(ANY, VMEM),
            scratch_shapes=[
                pltpu.VMEM((RING, OUT_ROWS, width), jnp.float32),
                pltpu.SemaphoreType.DMA((RING,)),
            ],
            compiler_params=pltpu.CompilerParams(vmem_limit_bytes=16 << 20),
            name="finish",
        )(pltpu.with_memory_space_constraint(prefix, pltpu.VMEM), coef, picked)
        return table, picked.reshape(rows)

    return jax.shard_map(
        local_step,
        mesh=mesh,
        in_specs=(P("dp", None), P(None, vocab_axes), P("dp"), P("dp")),
        out_specs=(P("dp", vocab_axes), P("dp")),
        check_vma=False,
    )
```

time: 202 us -> 59.4 us (0.29)
  local copies, waits for them, and re-layouts: 63 us -> 0.01 us
  Pallas kernels: 0 us -> 58.6 us
  other arithmetic: 47.2 us -> 0 us
  blocking collectives: 47.1 us -> 0 us
  matrix products: 43.4 us -> 0 us
    pallas_call x0 -> x3, Pallas kernels: none -> 58.6 us  [the longest x1 44.6 us: local_step(): pl.pallas_call(main_kernel, out_shape=(pltpu.VMEM((blocks, rows, BLOCK),...]
    dot_general x1 -> x0, matrix products: 43.4 us -> none  [local_step(): jnp.dot(hidden, w_head, preferred_element_type=jnp.float32)]
    unnamed x8 -> x4, local copies, waits for them, and re-layouts: 30.3 us -> 0.01 us
    all_gather x2 -> x0, blocking collectives: 24.8 us -> none  [the longest x1 13.9 us: local_step(): stat_pairs = lax.all_gather(jnp.stack([local_max, local_sum]), vocab_axes)]
    psum x1 -> x0, blocking collectives: 22.3 us -> none  [local_step(): lax.psum(jnp.sum(jnp.where(is_target, cdf_table, 0.0), axis=1), vocab_axes)]
    another operation x3 -> x0, other arithmetic: 19.3 us -> none
    reshape x1 -> x0, local copies, waits for them, and re-layouts: 16.5 us -> none
    another operation x3 -> x0, local copies, waits for them, and re-layouts: 15.7 us -> none
where the time goes in v1:
time: 59.4 us; the launch traced here: 59.3 us
  Pallas kernels  58.6 us (99%)
  between operations  0.68 us (1%)
    pallas_call x1, Pallas kernels, local_step(): pl.pallas_call(main_kernel, out_shape=(pltpu.VMEM((blocks, rows, BLOCK),...  44.6 us
    pallas_call x1, Pallas kernels, local_step(): pl.pallas_call(functools.partial(exchange_kernel, width), out_shape=(pltp...  7.25 us
    pallas_call x1, Pallas kernels, local_step(): pl.pallas_call(finish_kernel, out_shape=(jax.ShapeDtypeStruct((rows, widt...  6.74 us

profile of v1, /device:TPU:0, one launch (start us, length us, event | category | flops | bytes accessed | tf_op | source)
XLA Modules:
  0.0 59.3 jit_solution(3339222988543406633)
XLA Ops:
  0.6 0.0 copy-start
  0.6 0.0 copy-start.1
  0.7 44.6 %logits_prefix.1 = (f32[8,1024,512]{2,1,0:T(8,128)S(1)}, f32[3,8,1024]{2,1,0:T(8,128)S(1)}) custom-call(bf16[1024,4096]{1,0:T(8,128)(2,1)} %h_hbm.1, bf16[4096,4096]{1,0:T(8,128)(2,1)} %w_hbm.1, f32[1,1024]{1,0:T(1,128)} %bitcast.3, s32[1,1024]{1,0:T(1,128)} %bitcast.5), custom_call_target="tpu_custom_call" | custom-call | tf_op jit(solution)/shard_map/logits_prefix/pallas_call | solution.py:226
  45.3 0.0 copy-done
  45.3 0.0 copy-done.1
  45.3 7.2 %exchange.1 = (f32[1024,128]{1,0:T(8,128)S(1)}, f32[8,128]{1,0:T(8,128)S(1)}) custom-call(f32[3,8,1024]{2,1,0:T(8,128)S(1)} %get-tuple-element.9.stats, f32[1,1024]{1,0:T(1,128)S(1)} %bitcast.4, s32[1,1024]{1,0:T(1,128)S(1)} %bitcast.6), custom_call_target="tpu_custom_call" | custom-call | tf_op jit(solution)/shard_map/exchange/pallas_call | solution.py:247
  52.5 6.7 %finish.1 = (f32[1024,4096]{1,0:T(8,128)}, f32[8,128]{1,0:T(8,128)}) custom-call(f32[8,1024,512]{2,1,0:T(8,128)S(1)} %get-tuple-element.8.prefix, f32[1024,128]{1,0:T(8,128)S(1)} %get-tuple-element.10.coef, f32[8,128]{1,0:T(8,128)S(1)} %get-tuple-element.11.picked), custom_call_target="tpu_custom_call" | custom-call | tf_op jit(solution)/shard_map/finish/pallas_call | solution.py:266
Async XLA Ops:
  0.6 44.6 %copy-start = (f32[1024]{0:T(1024)S(1)}, f32[1024]{0:T(1024)}, u32[]{:S(2)}) copy-start(f32[1024]{0:T(1024)} %param.6) | copy-start | bytes 12292
  0.6 44.6 %copy-start.1 = (s32[1024]{0:T(1024)S(1)}, s32[1024]{0:T(1024)}, u32[]{:S(2)}) copy-start(s32[1024]{0:T(1024)} %param.7) | copy-start | bytes 12292
